TPU v7x, 32 devices: a whole 2x2x4 slice. The times are simulated.
32 devices in a mesh: row: 4 (over x, core), col: 8 (over z, y).
Axes of the slice: x: 2, y: 2, z: 4, core: 2. Of those that a mesh axis runs over, the one named last changes fastest.
Arguments:
- points: float32 [16, 8192], P(None, ('row', 'col')), may hold values from -6 to 6
- lengthscale: float32 [16], replicated, may hold values from 2 to 8
- signal: float32 [1], replicated, may hold values from 0.5 to 2
- noise: float32 [1], replicated, may hold values from 0.05 to 0.5
- targets: float32 [8192], P(('row', 'col')), may hold values from -12 to 12
- probe_bits: int32 [31, 8192], P(None, ('row', 'col')), may hold values from 0 to 1
Outputs:
- solution: float32 [32, 8192], P(None, ('row', 'col'))
- residual: float32 [32, 8192], P(None, ('row', 'col'))
All inputs are finite; a program needn't handle non-finite values.
Results may differ from a plain program's by a relative error of at most 0.0013.
Values sent between devices are 32-bit elements; how exact they have to be, the bound alone decides.
A program may use at most 128 MiB of HBM per device.

v0:
```python
import jax
import jax.numpy as jnp
from jax import lax
from jax.sharding import PartitionSpec as P

ITERS = 3


ROOT_FIVE = 5.0**0.5


def matern_tile(row_scaled, col_scaled, signal_value):
    row_sq = jnp.sum(row_scaled * row_scaled, axis=0)
    col_sq = jnp.sum(col_scaled * col_scaled, axis=0)
    cross_term = lax.dot_general(
        row_scaled,
        col_scaled,
        (((0,), (0,)), ((), ())),
        precision=lax.Precision.HIGHEST,
        preferred_element_type=jnp.float32,
    )
    dist_sq = jnp.maximum(row_sq[:, None] + col_sq[None, :] - 2.0 * cross_term, 0.0)
    radius = jnp.sqrt(dist_sq)
    return (
        signal_value
        * (1.0 + ROOT_FIVE * radius + 5.0 / 3.0 * dist_sq)
        * jnp.exp(-ROOT_FIVE * radius)
    )


def row_blocks(row_scaled):
    row_total = row_scaled.shape[1]
    block_rows = min(1024, row_total)
    block_count = row_total // block_rows
    return row_scaled.reshape(row_scaled.shape[0], block_count, block_rows).transpose(1, 0, 2)


def apply_tile(row_scaled, col_scaled, signal_value, vectors):
    row_total = row_scaled.shape[1]
    stacked = row_blocks(row_scaled)

    def one_block(row_block):
        kernel_tile = matern_tile(row_block, col_scaled, signal_value)
        return lax.dot_general(
            vectors,
            kernel_tile,
            (((1,), (1,)), ((), ())),
            precision=lax.Precision.HIGHEST,
            preferred_element_type=jnp.float32,
        )

    pieces = lax.map(one_block, stacked)
    return pieces.transpose(1, 0, 2).reshape(vectors.shape[0], row_total)


def squares(residual):
    return lax.psum(jnp.sum(residual * residual, axis=1), ("row", "col"))


def body(points, lengthscale, signal, noise, targets, probe_bits):
    scaled = points / lengthscale[:, None]
    signs = 2.0 * probe_bits.astype(jnp.float32) - 1.0
    right_side = jnp.concatenate([targets[None, :], signs], axis=0)
    signal_value = signal[0]
    noise_value = noise[0]
    every_point = lax.all_gather(scaled, ("row", "col"), axis=1, tiled=True)
    solution = jnp.zeros_like(right_side)
    residual = right_side
    direction = right_side
    norm_now = squares(residual)
    for step in range(ITERS):
        summed = apply_tile(
            scaled,
            every_point,
            signal_value,
            lax.all_gather(direction, ("row", "col"), axis=1, tiled=True),
        )
        image = summed + noise_value * direction
        curved = lax.psum(jnp.sum(direction * image, axis=1), ("row", "col"))
        alpha = norm_now / curved
        solution = solution + alpha[:, None] * direction
        residual = residual - alpha[:, None] * image
        if step + 1 < ITERS:
            norm_next = squares(residual)
            direction = residual + (norm_next / norm_now)[:, None] * direction
            norm_now = norm_next
    return (solution, residual)


def solution(mesh):
    return jax.shard_map(
        body,
        mesh=mesh,
        in_specs=(
            P(None, ("row", "col")),
            P(),
            P(),
            P(),
            P(("row", "col")),
            P(None, ("row", "col")),
        ),
        out_specs=(P(None, ("row", "col")), P(None, ("row", "col"))),
        check_vma=False,
    )
```

profile of v0, /device:TPU:0, one launch (start us, length us, event | category | flops | bytes accessed | tf_op | source)
XLA Modules:
  0.0 442.8 jit_solution(3945853298160864915)
XLA Ops:
  7.2 0.0 all-gather.4.cloned.1.call-start
  7.2 0.8 multiply_add_fusion.3
  8.0 1.3 pad_maximum_fusion
  9.3 0.0 all-gather.4.cloned.1.call-update
  9.3 0.0 all-gather.6.cloned.1.call-start
  10.6 0.8 multiply_reduce_fusion.7
  11.5 73.2 %all_gather.13 = f32[16,8192]{1,0:T(8,128)S(1)} all-gather(f32[16,256]{1,0:T(8,128)S(1)} %get-tuple-element.51), channel_id=1, replica_groups=mesh['row'=4,'col'=8] {'row','col'}, dimensions={1}, use_global_device_ids=true | all-gather | bytes 540672 | tf_op jit(solution)/shard_map/all_gather | solution.py:66
  84.6 0.1 multiply_reduce_fusion
  84.7 0.0 copy-start.2
  84.7 14.0 %exponential_multiply_fusion = f32[256,8192]{1,0:T(8,128)} fusion(f32[16,256]{1,0:T(8,128)S(1)} %get-tuple-element.51, f32[16,8192]{1,0:T(8,128)S(1)} %all_gather.13, f32[8192]{0:T(1024)S(1)} %multiply_reduce_fusion, f32[256]{0:T(256)S(1)} %get-tuple-element.50, f32[]{:T(128)} %bitcast.11), kind=kOutput, calls=%fused_computation.3 | convolution fusion | flops 425721856 | bytes 8963076 | tf_op jit(solution)/shard_map/while/body/eval_jaxpr/dot_general | solution.py:15
  98.7 0.0 copy-done.2
  98.8 11.2 %multiply_reduce_fusion.5 = (f32[32]{0:T(128)S(1)}, f32[32]{0:T(128)S(1)}, f32[32,256]{1,0:T(8,128)S(1)}) fusion(f32[32,256]{1,0:T(8,128)S(1)} %copy-done.2, f32[]{:T(128)} %bitcast.12, f32[32,8192]{1,0:T(8,128)} %all-gather.4.cloned.1.call-done, f32[256,8192]{1,0:T(8,128)} %exponential_multiply_fusion), kind=kOutput, calls=%fused_computation.19 | convolution fusion | flops 805355456 | bytes 9502980 | tf_op jit(solution)/shard_map/while/body/eval_jaxpr/dot_general | solution.py:44
  109.9 37.1 %all-reduce = (f32[32]{0:T(128)S(1)}, f32[32]{0:T(128)S(1)}) all-reduce(f32[32]{0:T(128)S(1)} %get-tuple-element.39, f32[32]{0:T(128)S(1)} %get-tuple-element.38), channel_id=1, replica_groups=mesh['row'=4,'col'=8] {'row','col'}, use_global_device_ids=true, to_apply=%region_1.0 | all-reduce | flops 64 | bytes 512 | tf_op jit(solution)/shard_map/psum | solution.py:57
  147.0 0.0 copy-done.3
  147.0 0.2 multiply_reduce_fusion.4
  147.2 41.5 %psum.44 = f32[32]{0:T(128)S(1)} all-reduce(f32[32]{0:T(128)S(1)} %multiply_reduce_fusion.4), channel_id=1, replica_groups=mesh['row'=4,'col'=8] {'row','col'}, use_global_device_ids=true, to_apply=%region_7.8 | all-reduce | flops 32 | bytes 256 | tf_op jit(solution)/shard_map/psum | solution.py:57
  188.7 0.7 multiply_add_fusion.2
  189.4 0.0 all-gather.6.cloned.1.call-update
  189.5 0.0 all-gather.8.cloned.1.call-start
  189.5 51.3 %all-gather.6.cloned.1.call-done = f32[32,8192]{1,0:T(8,128)} async-done(((f32[32,256]{1,0:T(8,128)}), f32[32,8192]{1,0:T(8,128)}) %all-gather.6.cloned.1.call-update) | async-done | bytes 1048592 | tf_op jit(solution)/shard_map/all_gather | solution.py:76
  240.8 11.1 %multiply_reduce_fusion.3 = (f32[32]{0:T(128)S(1)}, f32[32,256]{1,0:T(8,128)S(1)}) fusion(f32[32,256]{1,0:T(8,128)} %multiply_add_fusion.2, f32[]{:T(128)} %bitcast.14, f32[32,8192]{1,0:T(8,128)} %all-gather.6.cloned.1.call-done, f32[256,8192]{1,0:T(8,128)} %exponential_multiply_fusion), kind=kOutput, calls=%fused_computation.15 | convolution fusion | flops 805339136 | bytes 9502852 | tf_op jit(solution)/shard_map/while/body/eval_jaxpr/dot_general | solution.py:44
  251.9 40.3 %psum.45 = f32[32]{0:T(128)S(1)} all-reduce(f32[32]{0:T(128)S(1)} %get-tuple-element.61), channel_id=1, replica_groups=mesh['row'=4,'col'=8] {'row','col'}, use_global_device_ids=true, to_apply=%region_9.10 | all-reduce | flops 32 | bytes 256 | tf_op jit(solution)/shard_map/psum | solution.py:79
  292.1 0.2 multiply_reduce_fusion.2
  292.3 39.2 %psum.46 = f32[32]{0:T(128)S(1)} all-reduce(f32[32]{0:T(128)S(1)} %get-tuple-element.48), channel_id=1, replica_groups=mesh['row'=4,'col'=8] {'row','col'}, use_global_device_ids=true, to_apply=%region_11.12 | all-reduce | flops 32 | bytes 256 | tf_op jit(solution)/shard_map/psum | solution.py:57
  331.5 0.0 copy-done
  331.5 0.7 multiply_add_fusion.1
  332.2 0.0 all-gather.8.cloned.1.call-update
  332.3 52.0 %all-gather.8.cloned.1.call-done = f32[32,8192]{1,0:T(8,128)} async-done(((f32[32,256]{1,0:T(8,128)}), f32[32,8192]{1,0:T(8,128)}) %all-gather.8.cloned.1.call-update) | async-done | bytes 1048592 | tf_op jit(solution)/shard_map/all_gather | solution.py:76
  384.2 11.1 %multiply_reduce_fusion.1 = (f32[32]{0:T(128)S(1)}, f32[32,256]{1,0:T(8,128)S(1)}) fusion(f32[32,256]{1,0:T(8,128)} %multiply_add_fusion.1, f32[]{:T(128)} %bitcast.13, f32[32,8192]{1,0:T(8,128)} %all-gather.8.cloned.1.call-done, f32[256,8192]{1,0:T(8,128)} %exponential_multiply_fusion), kind=kOutput, calls=%fused_computation.11 | convolution fusion | flops 805339136 | bytes 9502852 | tf_op jit(solution)/shard_map/while/body/eval_jaxpr/dot_general | solution.py:44
  395.3 40.3 %psum.47 = f32[32]{0:T(128)S(1)} all-reduce(f32[32]{0:T(128)S(1)} %get-tuple-element.63), channel_id=1, replica_groups=mesh['row'=4,'col'=8] {'row','col'}, use_global_device_ids=true, to_apply=%region_13.14 | all-reduce | flops 32 | bytes 256 | tf_op jit(solution)/shard_map/psum | solution.py:79
  435.5 0.0 copy-done.1
  435.5 0.7 multiply_subtract_fusion
  (9 shorter events, 0.0 us)
Async XLA Ops:
  7.2 91.6 %all-gather.4.cloned.1.call-start = ((), (), s32[]{:S(2)}) async-start(), calls=%async_computation | async-start | bytes 1081344 | tf_op jit(solution)/shard_map/all_gather | solution.py:76
  9.3 231.5 %all-gather.6.cloned.1.call-start = ((), (), s32[]{:S(2)}) async-start(), calls=%async_computation.1 | async-start | bytes 1081344 | tf_op jit(solution)/shard_map/all_gather | solution.py:76
  84.7 14.0 %copy-start.2 = (f32[32,256]{1,0:T(8,128)S(1)}, f32[32,256]{1,0:T(8,128)}, u32[]{:S(2)}) copy-start(f32[32,256]{1,0:T(8,128)} %pad_maximum_fusion) | copy-start | bytes 98308
  98.7 48.3 %copy-start.3 = (f32[256]{0:T(256)S(1)}, f32[256]{0:T(256)}, u32[]{:S(2)}) copy-start(f32[256]{0:T(256)} %param.10) | copy-start | bytes 3076
  189.4 142.1 %copy-start = (f32[32,256]{1,0:T(8,128)S(1)}, f32[32,256]{1,0:T(8,128)}, u32[]{:S(2)}) copy-start(f32[32,256]{1,0:T(8,128)} %multiply_add_fusion.2) | copy-start | bytes 98308
  189.5 194.7 %all-gather.8.cloned.1.call-start = ((), (), s32[]{:S(2)}) async-start(), calls=%async_computation.2 | async-start | bytes 1081344 | tf_op jit(solution)/shard_map/all_gather | solution.py:76
  332.2 103.3 %copy-start.1 = (f32[32,256]{1,0:T(8,128)S(1)}, f32[32,256]{1,0:T(8,128)}, u32[]{:S(2)}) copy-start(f32[32,256]{1,0:T(8,128)} %multiply_add_fusion.1) | copy-start | bytes 98308
Sparse Core Ops, SparseCore 0:
  11.4 54.6 all-gather.3
  189.6 51.1 all-gather.5
  332.4 51.7 all-gather.7
where the time goes:
time: 444 us; the launch traced here: 443 us
  blocking collectives  272 us (61%)
  waiting for transfers between devices  103 us (23%)
  matrix products  47.3 us (11%)
  between operations  15.1 us (3%)
  other arithmetic  5.46 us (1%)
    psum x3, blocking collectives, squares(): return lax.psum(jnp.sum(residual * residual, axis=1), ('row', 'col'))  118 us
    all_gather x3, waiting for transfers between devices, body(): lax.all_gather(direction, ('row', 'col'), axis=1, tiled=True)  103 us
    psum x2, blocking collectives, body(): curved = lax.psum(jnp.sum(direction * image, axis=1), ('row', 'col'))  80.5 us
    all_gather x1, blocking collectives, body(): every_point = lax.all_gather(scaled, ('row', 'col'), axis=1, tiled=True)  73.2 us
    dot_general x3, matrix products, one_block(): lax.dot_general(vectors, kernel_tile, (((1,), (1,)), ((), ())), precision...  33.3 us
    dot_general x1, matrix products, matern_tile(): lax.dot_general(row_scaled, col_scaled, (((0,), (0,)), ((), ())), precisi...  14 us
  transfers between devices with their start and end apart: 3, of which 2 were waited for; matrix products, arithmetic and copies ran while one was open for 3% of the time, Pallas kernels for 0%

commit v1 on v0

v1 whole, which is shorter than its diff:
```python
import functools
import math

import jax
import jax.numpy as jnp
from jax import lax
from jax.experimental import pallas as pl
from jax.experimental.pallas import tpu as pltpu
from jax.sharding import PartitionSpec as P

ITERS = 3
MESH = pl.DeviceIdType.MESH
LOG2E = math.log2(math.e)
POINT_SCALE = math.sqrt(5.0) * LOG2E
POINTS, RIGHT, IMAGE0, IMAGE1 = range(4)


def split(value, count):
    parts = []
    for _ in range(count):
        part = value.astype(jnp.bfloat16)
        parts.append(part)
        value = value - part.astype(jnp.float32)
    return parts


def norm_rows(points, first):
    norm = jnp.sum(points * points, axis=0, keepdims=True)
    n1, n2, n3 = [part.astype(jnp.float32) for part in split(norm, 3)]
    row = lax.broadcasted_iota(jnp.int32, points.shape, 0)
    base = 0 if first else 3
    ones = 3 - base
    rows = jnp.where((row >= ones) & (row < ones + 3), 1.0, 0.0)
    for place, part in enumerate((n1, n2, n3)):
        rows = jnp.where(row == base + place, part, rows)
    return rows.astype(jnp.bfloat16)


def left_stack(points):
    s1, s2, s3 = split(points, 3)
    return jnp.concatenate([s1, s1, s2, s2, s1, s3, norm_rows(points, True)], axis=0)


def right_stack(points):
    s1, s2, s3 = split(-2.0 * points, 3)
    return jnp.concatenate([s1, s2, s1, s2, s3, s1, norm_rows(points, False)], axis=0)


def kernel_body(
    rows, cols,
    points_ref, length_ref, signal_ref, noise_ref, targets_ref, bits_ref,
    solution_ref, residual_ref,
    pts, vec, im0, im1, halves, khi, klo, scal, own_right,
    send_peer, recv_peer, send_sib, recv_sib, send_scal, recv_scal,
):
    devices = rows * cols
    chips = devices // 2
    width = points_ref.shape[1]
    count = bits_ref.shape[0] + 1
    row = lax.axis_index("row")
    col = lax.axis_index("col")
    core = lax.rem(row, 2)
    me = row * cols + col
    chip = lax.div(row, 2) * cols + col
    buffers = (pts, vec, im0, im1)

    def slot_of(chip_index, core_index):
        high = lax.div(chip_index, cols)
        return (2 * high + core_index) * cols + lax.rem(chip_index, cols)

    def chip_id(chip_index, core_index):
        return (2 * lax.div(chip_index, cols) + core_index, lax.rem(chip_index, cols))

    def to_peer(phase, k):
        return pltpu.make_async_remote_copy(
            src_ref=buffers[phase].at[me],
            dst_ref=buffers[phase].at[me],
            send_sem=send_peer.at[phase, k],
            recv_sem=recv_peer.at[phase, k],
            device_id=chip_id(lax.rem(chip + k, chips), core),
            device_id_type=MESH,
        )

    def source(k):
        return lax.rem(chip + chips - k, chips)

    def to_sibling(phase, k):
        slot = slot_of(source(k), core)
        return pltpu.make_async_remote_copy(
            src_ref=buffers[phase].at[slot],
            dst_ref=buffers[phase].at[slot],
            send_sem=send_sib.at[phase, k],
            recv_sem=recv_sib.at[phase, k],
            device_id=(row + 1 - 2 * core, col),
            device_id_type=MESH,
        )

    def each(low, high, step):
        def run(k, carry):
            step(k)
            return carry

        lax.fori_loop(low, high, run, 0)

    def send_all(phase):
        each(1, chips, lambda k: to_peer(phase, k).start())
        to_sibling(phase, 0).start()

    def sent_all(phase):
        each(1, chips, lambda k: to_peer(phase, k).wait_send())
        each(0, chips, lambda k: to_sibling(phase, k).wait_send())

    def arrive_peer(phase, k):
        to_peer(phase, k).wait_recv()
        to_sibling(phase, k).start()

    diagonal = lax.broadcasted_iota(jnp.int32, (points_ref.shape[0],) * 2, 0) == lax.broadcasted_iota(
        jnp.int32, (points_ref.shape[0],) * 2, 1
    )
    length = jnp.sum(jnp.where(diagonal, length_ref[...], 0.0), axis=1, keepdims=True)
    mine = points_ref[...] / length * POINT_SCALE
    pts[me] = mine
    own_right[0:1, :] = targets_ref[...]
    own_right[1:count, :] = 2.0 * bits_ref[...].astype(jnp.float32) - 1.0
    vec[me] = own_right[...]

    barrier = pltpu.get_barrier_semaphore()

    def greet(k):
        other = lax.rem(me + k, devices)
        pl.semaphore_signal(
            barrier, inc=1, device_id=(lax.div(other, cols), lax.rem(other, cols)), device_id_type=MESH
        )

    each(1, devices, greet)
    pl.semaphore_wait(barrier, devices - 1)

    send_all(POINTS)
    send_all(RIGHT)

    signal = signal_ref[0]
    noise = noise_ref[0]
    c1 = signal * (1.0 / LOG2E)
    c2 = signal * (1.0 / (3.0 * LOG2E * LOG2E))
    across = right_stack(mine)

    def kernel_tile(slot):
        down = left_stack(pts[slot])
        square = lax.dot_general(
            down, across, (((0,), (0,)), ((), ())), preferred_element_type=jnp.float32
        )
        square = jnp.maximum(square, 1e-30)
        w = square * lax.rsqrt(square)
        tile = (signal + c1 * w + c2 * square) * jnp.exp2(-w)
        high = tile.astype(jnp.bfloat16)
        place = pl.ds(pl.multiple_of(slot * width, width), width)
        khi[place, :] = high
        klo[place, :] = (tile - high.astype(jnp.float32)).astype(jnp.bfloat16)

    kernel_tile(me)

    def peer_tile(k):
        arrive_peer(POINTS, k)
        kernel_tile(slot_of(source(k), core))

    each(1, chips, peer_tile)
    each(1, chips, lambda k: arrive_peer(RIGHT, k))

    def sibling_tile(k):
        to_sibling(POINTS, k).wait_recv()
        kernel_tile(slot_of(source(k), 1 - core))

    each(0, chips, sibling_tile)
    each(0, chips, lambda k: to_sibling(RIGHT, k).wait_recv())
    sent_all(POINTS)
    sent_all(RIGHT)

    zero = jnp.zeros((count, width), jnp.float32)

    def total(value):
        return jnp.sum(value, axis=1, keepdims=True)

    def put_halves(j, value):
        high = value.astype(jnp.bfloat16)
        place = pl.ds(pl.multiple_of(j * width, width), width)
        halves[0:count, place] = high
        halves[count : 2 * count, place] = (value - high.astype(jnp.float32)).astype(jnp.bfloat16)

    def first_pass(j, carry):
        value = vec[j]
        put_halves(j, value)
        return carry + value * value

    norm_now = total(lax.fori_loop(0, devices, first_pass, zero))

    def image():
        both = jnp.dot(halves[...], khi[...], preferred_element_type=jnp.float32)
        rest = jnp.dot(halves[0:count, :], klo[...], preferred_element_type=jnp.float32)
        return both[:count] + (both[count:] + rest) + noise * vec[me]

    solved = zero
    residuals = vec
    for step in range(ITERS - 1):
        phase = IMAGE0 + step
        images = buffers[phase]
        images[me] = image()
        send_all(phase)

        def from_peer(k, carry):
            arrive_peer(phase, k)
            slot = slot_of(source(k), core)
            return carry + vec[slot] * images[slot]

        def from_sibling(k, carry):
            to_sibling(phase, k).wait_recv()
            slot = slot_of(source(k), 1 - core)
            return carry + vec[slot] * images[slot]

        curved = vec[me] * images[me]
        curved = lax.fori_loop(1, chips, from_peer, curved)
        curved = lax.fori_loop(0, chips, from_sibling, curved)
        sent_all(phase)
        alpha = norm_now / total(curved)
        solved = solved + alpha * vec[me]

        def reduce_pass(j, carry):
            value = residuals[j] - alpha * images[j]
            images[j] = value
            return carry + value * value

        norm_next = total(lax.fori_loop(0, devices, reduce_pass, zero))
        beta = norm_next / norm_now
        norm_now = norm_next

        def turn_pass(j, carry):
            value = images[j] + beta * vec[j]
            vec[j] = value
            put_halves(j, value)
            return carry

        lax.fori_loop(0, devices, turn_pass, 0)
        residuals = images

    last = image()
    part = total(vec[me] * last)
    square_shape = (count, 128)
    on_diagonal = lax.broadcasted_iota(jnp.int32, square_shape, 0) == lax.broadcasted_iota(
        jnp.int32, square_shape, 1
    )
    line = jnp.sum(jnp.where(on_diagonal, part, 0.0), axis=0, keepdims=True)
    scal[me] = jnp.broadcast_to(line, scal.shape[1:])

    def scalar_copy(k):
        other = lax.rem(me + k, devices)
        return pltpu.make_async_remote_copy(
            src_ref=scal.at[me],
            dst_ref=scal.at[me],
            send_sem=send_scal.at[k],
            recv_sem=recv_scal.at[k],
            device_id=(lax.div(other, cols), lax.rem(other, cols)),
            device_id_type=MESH,
        )

    each(1, devices, lambda k: scalar_copy(k).start())
    each(1, devices, lambda k: scalar_copy(k).wait_recv())
    summed = lax.fori_loop(1, devices, lambda j, carry: carry + scal[j], scal[0])
    curved = total(jnp.where(on_diagonal, summed[0:1, :], 0.0))
    alpha = norm_now / curved
    solution_ref[...] = solved + alpha * vec[me]
    residual_ref[...] = residuals[me] - alpha * last
    each(1, devices, lambda k: scalar_copy(k).wait_send())


def solution(mesh):
    rows, cols = mesh.shape["row"], mesh.shape["col"]
    devices = rows * cols
    chips = devices // 2

    def body(points, lengthscale, signal, noise, targets, probe_bits):
        dims, width = points.shape
        count = probe_bits.shape[0] + 1
        block = jax.ShapeDtypeStruct((count, width), jnp.float32)
        vmem = pl.BlockSpec(memory_space=pltpu.VMEM)
        smem = pl.BlockSpec(memory_space=pltpu.SMEM)
        slots = pltpu.VMEM((devices, count, width), jnp.float32)
        return pl.pallas_call(
            functools.partial(kernel_body, rows, cols),
            out_shape=(block, block),
            in_specs=[vmem, vmem, smem, smem, vmem, vmem],
            out_specs=(vmem, vmem),
            scratch_shapes=[
                pltpu.VMEM((devices, dims, width), jnp.float32),
                slots,
                slots,
                slots,
                pltpu.VMEM((2 * count, devices * width), jnp.bfloat16),
                pltpu.VMEM((devices * width, width), jnp.bfloat16),
                pltpu.VMEM((devices * width, width), jnp.bfloat16),
                pltpu.VMEM((devices, 8, 128), jnp.float32),
                pltpu.VMEM((count, width), jnp.float32),
                pltpu.SemaphoreType.DMA((4, chips)),
                pltpu.SemaphoreType.DMA((4, chips)),
                pltpu.SemaphoreType.DMA((4, chips)),
                pltpu.SemaphoreType.DMA((4, chips)),
                pltpu.SemaphoreType.DMA((devices,)),
                pltpu.SemaphoreType.DMA((devices,)),
            ],
            compiler_params=pltpu.CompilerParams(
                collective_id=0, has_side_effects=True, vmem_limit_bytes=60 * 1024 * 1024
            ),
        )(points, lengthscale[None, :], signal, noise, targets[None, :], probe_bits)

    split_points = P(None, ("row", "col"))
    return jax.shard_map(
        body,
        mesh=mesh,
        in_specs=(split_points, P(), P(), P(), P(("row", "col")), split_points),
        out_specs=(split_points, split_points),
        check_vma=False,
    )
```

time: 444 us -> 83.8 us (0.19)
  blocking collectives: 272 us -> 0 us
  waiting for transfers between devices: 103 us -> 0 us
  Pallas kernels: 0 us -> 79.6 us
  matrix products: 47.3 us -> 0 us
  between operations: 15.1 us -> 1.94 us
  other arithmetic: 5.46 us -> 0 us
    psum x5 -> x0, blocking collectives: 198 us -> none  [the longest x3 118 us: squares(): return lax.psum(jnp.sum(residual * residual, axis=1), ('row', 'col'))]
    all_gather x3 -> x0, waiting for transfers between devices: 103 us -> none  [body(): lax.all_gather(direction, ('row', 'col'), axis=1, tiled=True)]
    pallas_call x0 -> x1, Pallas kernels: none -> 79.6 us  [body(): pl.pallas_call(functools.partial(kernel_body, rows, cols), out_shape=(blo...]
    all_gather x1 -> x0, blocking collectives: 73.2 us -> none  [body(): every_point = lax.all_gather(scaled, ('row', 'col'), axis=1, tiled=True)]
    dot_general x4 -> x0, matrix products: 47.3 us -> none  [the longest x3 33.3 us: one_block(): lax.dot_general(vectors, kernel_tile, (((1,), (1,)), ((), ())), precision...]
  transfers between devices with their start and end apart: 3 -> 0, of which waited for: 2 -> 0; matrix products, arithmetic and copies ran while one was open for 3% -> 0% of each run, Pallas kernels for 0% -> 0%
where the time goes in v1:
time: 83.8 us; the launch traced here: 83.5 us
  Pallas kernels  79.6 us (95%)
  local copies, waits for them, and re-layouts  2 us (2%)
  between operations  1.94 us (2%)
    pallas_call x1, Pallas kernels, body(): pl.pallas_call(functools.partial(kernel_body, rows, cols), out_shape=(blo...  79.6 us
    unnamed x4, local copies, waits for them, and re-layouts  2 us

profile of v1, /device:TPU:0, one launch (start us, length us, event | category | flops | bytes accessed | tf_op | source)
XLA Modules:
  0.0 83.5 jit_solution(15494724927073775120)
XLA Ops:
  1.9 79.6 %shard_map.77 = (f32[32,256]{1,0:T(8,128)}, f32[32,256]{1,0:T(8,128)}) custom-call(f32[16,256]{1,0:T(8,128)} %points_ref.1, f32[1,16]{1,0:T(1,128)} %bitcast.3, f32[1]{0:T(128)S(6)} %copy.10.signal_ref, f32[1]{0:T(128)S(6)} %copy.11.noise_ref, f32[1,256]{1,0:T(1,128)} %bitcast.2, s32[31,256]{1,0:T(8,128)} %bits_ref.1), custom_call_target="tpu_custom_call" | custom-call | tf_op jit(solution)/shard_map/pallas_call | solution.py:286
  81.5 0.0 copy-start
  81.5 1.4 %copy.12 = f32[32,256]{1,0:T(8,128)} copy(f32[32,256]{1,0:T(8,128)} %get-tuple-element.4) | data formatting | bytes 65536
  82.9 0.0 copy-done
  82.9 0.6 copy.13
Async XLA Ops:
  81.5 1.4 %copy-start = (f32[32,256]{1,0:T(8,128)S(1)}, f32[32,256]{1,0:T(8,128)}, u32[]{:S(2)}) copy-start(f32[32,256]{1,0:T(8,128)} %get-tuple-element.5) | copy-start | bytes 98308

commit v2 on v1

v2 whole, which is shorter than its diff:
```python
import functools
import math

import jax
import jax.numpy as jnp
from jax import lax
from jax.experimental import pallas as pl
from jax.experimental.pallas import tpu as pltpu
from jax.sharding import PartitionSpec as P

ITERS = 3
MESH = pl.DeviceIdType.MESH
LOG2E = math.log2(math.e)
POINT_SCALE = math.sqrt(5.0) * LOG2E
POINTS, RIGHT, IMAGE0, IMAGE1 = range(4)


def split(value, count):
    parts = []
    for _ in range(count):
        part = value.astype(jnp.bfloat16)
        parts.append(part)
        value = value - part.astype(jnp.float32)
    return parts


def norm_rows(points, first):
    norm = jnp.sum(points * points, axis=0, keepdims=True)
    n1, n2, n3 = [part.astype(jnp.float32) for part in split(norm, 3)]
    row = lax.broadcasted_iota(jnp.int32, points.shape, 0)
    base = 0 if first else 3
    ones = 3 - base
    rows = jnp.where((row >= ones) & (row < ones + 3), 1.0, 0.0)
    for place, part in enumerate((n1, n2, n3)):
        rows = jnp.where(row == base + place, part, rows)
    return rows.astype(jnp.bfloat16)


def left_stack(points):
    s1, s2, s3 = split(points, 3)
    return jnp.concatenate([s1, s1, s2, s2, s1, s3, norm_rows(points, True)], axis=0)


def right_stack(points):
    s1, s2, s3 = split(-2.0 * points, 3)
    return jnp.concatenate([s1, s2, s1, s2, s3, s1, norm_rows(points, False)], axis=0)


def kernel_body(
    rows, cols,
    points_ref, length_ref, signal_ref, noise_ref, targets_ref, bits_ref,
    solution_ref, residual_ref,
    pts, vec, im0, im1, khi, klo, scal,
    send_peer, recv_peer, send_sib, recv_sib, send_scal, recv_scal,
):
    devices = rows * cols
    chips = devices // 2
    width = points_ref.shape[1]
    count = bits_ref.shape[0] + 1
    wide = rows // 2
    minor = 1
    while 4 * minor * minor <= cols:
        minor *= 2
    major = cols // minor
    chunk = major
    chunks = chips // chunk
    row = lax.axis_index("row")
    col = lax.axis_index("col")
    core = lax.rem(row, 2)
    x = lax.div(row, 2)
    z = lax.div(col, minor)
    y = lax.rem(col, minor)
    turned = core if wide == minor else 0
    first, second = wide, minor
    buffers = (pts, vec, im0, im1)

    def parts_of(k):
        return k % major, k // major % first, k // major // first

    def device_at(dz, df, ds):
        tx = lax.rem(x + df + turned * (ds - df), wide)
        ty = lax.rem(y + ds + turned * (df - ds), minor)
        tz = lax.rem(z + dz, major)
        return (2 * tx + core, tz * minor + ty)

    sibling = (row + 1 - 2 * core, col)

    def to_peer(phase, k):
        dz, df, ds = parts_of(k)
        if ds > 0:
            held, target = k - ds * first * major, (0, 0, ds)
        elif df > 0:
            held, target = dz, (0, df, 0)
        else:
            held, target = 0, (dz, 0, 0)
        return pltpu.make_async_remote_copy(
            src_ref=buffers[phase].at[held],
            dst_ref=buffers[phase].at[k],
            send_sem=send_peer.at[phase, k],
            recv_sem=recv_peer.at[phase, k],
            device_id=device_at(*target),
            device_id_type=MESH,
        )

    def to_sibling(phase, k):
        return pltpu.make_async_remote_copy(
            src_ref=buffers[phase].at[k],
            dst_ref=buffers[phase].at[chips + k],
            send_sem=send_sib.at[phase, k],
            recv_sem=recv_sib.at[phase, k],
            device_id=sibling,
            device_id_type=MESH,
        )

    def pass_on(phase, k):
        dz, df, ds = parts_of(k)
        if k == 0:
            for j in range(1, major):
                to_peer(phase, j).start()
        if df == 0 and ds == 0:
            for j in range(1, first):
                to_peer(phase, k + j * major).start()
        if ds == 0:
            for j in range(1, second):
                to_peer(phase, k + j * first * major).start()
        to_sibling(phase, k).start()

    def forward(phase, c):
        for k in range(c * chunk, (c + 1) * chunk):
            if k > 0:
                to_peer(phase, k).wait_recv()
                pass_on(phase, k)

    def arrive_sibling(phase, c):
        for k in range(c * chunk, (c + 1) * chunk):
            to_sibling(phase, k).wait_recv()

    def sent_all(phase):
        for k in range(chips):
            if k > 0:
                to_peer(phase, k).wait_send()
            to_sibling(phase, k).wait_send()

    barrier = pltpu.get_barrier_semaphore()
    for k in range(1, chips):
        pl.semaphore_signal(barrier, inc=1, device_id=device_at(*parts_of(k)), device_id_type=MESH)
    pl.semaphore_signal(barrier, inc=1, device_id=sibling, device_id_type=MESH)

    diagonal = lax.broadcasted_iota(jnp.int32, (points_ref.shape[0],) * 2, 0) == lax.broadcasted_iota(
        jnp.int32, (points_ref.shape[0],) * 2, 1
    )
    length = jnp.sum(jnp.where(diagonal, length_ref[...], 0.0), axis=1, keepdims=True)
    mine = points_ref[...] / length * POINT_SCALE
    pts[0] = mine
    vec[0, 0:1, :] = targets_ref[...]
    vec[0, 1:count, :] = 2.0 * bits_ref[...].astype(jnp.float32) - 1.0

    signal = signal_ref[0]
    noise = noise_ref[0]
    c1 = signal * (1.0 / LOG2E)
    c2 = signal * (1.0 / (3.0 * LOG2E * LOG2E))
    across = right_stack(mine)

    pl.semaphore_wait(barrier, chips)
    pass_on(POINTS, 0)
    pass_on(RIGHT, 0)

    def kernel_tile(slot):
        down = left_stack(pts[slot])
        square = lax.dot_general(
            down, across, (((0,), (0,)), ((), ())), preferred_element_type=jnp.float32
        )
        square = jnp.maximum(square, 1e-30)
        w = square * lax.rsqrt(square)
        tile = (signal + c1 * w + c2 * square) * jnp.exp2(-w)
        high = tile.astype(jnp.bfloat16)
        place = pl.ds(pl.multiple_of(slot * width, width), width)
        khi[place, :] = high
        klo[place, :] = (tile - high.astype(jnp.float32)).astype(jnp.bfloat16)

    def kernel_tiles(start):
        def run(j, carry):
            kernel_tile(start + j)
            return carry

        lax.fori_loop(0, chunk, run, 0)

    for c in range(first):
        forward(POINTS, c)
    for c in range(chunks):
        kernel_tiles(c * chunk)
        forward(RIGHT, c)
        if first + c < chunks:
            forward(POINTS, first + c)
    for c in range(chunks):
        arrive_sibling(POINTS, c)
        kernel_tiles(chips + c * chunk)
    for c in range(chunks):
        arrive_sibling(RIGHT, c)

    zero = jnp.zeros((count, width), jnp.float32)

    def total(value):
        return jnp.sum(value, axis=1, keepdims=True)

    def over_blocks(step, carry):
        def run(j, carry):
            for i in range(4):
                carry = step(4 * j + i, carry)
            return carry

        return lax.fori_loop(0, devices // 4, run, carry)

    def multiply(buffer, start, blocks):
        highs, lows = [], []
        for i in range(blocks):
            value = buffer[start + i]
            high = value.astype(jnp.bfloat16)
            highs.append(high)
            lows.append((value - high.astype(jnp.float32)).astype(jnp.bfloat16))
        high = jnp.concatenate(highs, axis=1)
        both = jnp.concatenate([high, jnp.concatenate(lows, axis=1)], axis=0)
        place = pl.ds(start * width, blocks * width)
        if not isinstance(start, int):
            place = pl.ds(pl.multiple_of(start * width, blocks * width), blocks * width)
        product = jnp.dot(both, khi[place, :], preferred_element_type=jnp.float32)
        rest = jnp.dot(high, klo[place, :], preferred_element_type=jnp.float32)
        return product[:count] + (product[count:] + rest)

    group = min(8, devices)

    def right_step(j, carry):
        image, norm = carry
        for i in range(group):
            value = vec[j * group + i]
            norm = norm + value * value
        return image + multiply(vec, j * group, group), norm

    summed, norm = lax.fori_loop(0, devices // group, right_step, (zero, zero))
    norm_now = total(norm)
    of_residual = summed + noise * vec[0]
    of_direction = of_residual
    sent_all(POINTS)
    sent_all(RIGHT)

    solved = zero
    residuals = vec
    for step in range(ITERS - 1):
        phase = IMAGE0 + step
        images = buffers[phase]
        images[0] = of_direction
        pass_on(phase, 0)
        curved = zero
        product = noise * of_direction

        def consume(start, curved, product):
            for i in range(chunk):
                curved = curved + vec[start + i] * images[start + i]
            return curved, product + multiply(images, start, chunk)

        for c in range(first):
            forward(phase, c)
        for c in range(chunks):
            curved, product = consume(c * chunk, curved, product)
            if c > 0:
                arrive_sibling(phase, c - 1)
                curved, product = consume(chips + (c - 1) * chunk, curved, product)
            if first + c < chunks:
                forward(phase, first + c)
        arrive_sibling(phase, chunks - 1)
        curved, product = consume(chips + (chunks - 1) * chunk, curved, product)
        sent_all(phase)
        alpha = norm_now / total(curved)
        solved = solved + alpha * vec[0]

        def reduce_pass(j, carry):
            value = residuals[j] - alpha * images[j]
            images[j] = value
            return carry + value * value

        norm_next = total(over_blocks(reduce_pass, zero))
        beta = norm_next / norm_now
        norm_now = norm_next
        of_residual = of_residual - alpha * product
        of_direction = of_residual + beta * of_direction

        if step + 2 < ITERS:

            def turn_pass(j, carry):
                vec[j] = images[j] + beta * vec[j]
                return carry

            over_blocks(turn_pass, 0)
        else:
            vec[0] = images[0] + beta * vec[0]
        residuals = images

    part = total(vec[0] * of_direction)
    square_shape = (count, 128)
    on_diagonal = lax.broadcasted_iota(jnp.int32, square_shape, 0) == lax.broadcasted_iota(
        jnp.int32, square_shape, 1
    )
    scal[0] = jnp.sum(jnp.where(on_diagonal, part, 0.0), axis=0, keepdims=True)

    def scalar_copy(k):
        return pltpu.make_async_remote_copy(
            src_ref=scal.at[0 if k == 0 else 2],
            dst_ref=scal.at[1 if k == 0 else 2 + k],
            send_sem=send_scal.at[k],
            recv_sem=recv_scal.at[k],
            device_id=sibling if k == 0 else device_at(*parts_of(k)),
            device_id_type=MESH,
        )

    scalar_copy(0).start()
    scalar_copy(0).wait_recv()
    summed = scal[0] + scal[1]
    scal[2] = summed
    for k in range(1, chips):
        scalar_copy(k).start()
    for k in range(1, chips):
        scalar_copy(k).wait_recv()
    for k in range(1, chips):
        summed = summed + scal[2 + k]
    curved = total(jnp.where(on_diagonal, summed, 0.0))
    alpha = norm_now / curved
    solution_ref[...] = solved + alpha * vec[0]
    residual_ref[...] = residuals[0] - alpha * of_direction
    for k in range(chips):
        scalar_copy(k).wait_send()


def solution(mesh):
    rows, cols = mesh.shape["row"], mesh.shape["col"]
    devices = rows * cols
    chips = devices // 2

    def body(points, lengthscale, signal, noise, targets, probe_bits):
        dims, width = points.shape
        count = probe_bits.shape[0] + 1
        block = jax.ShapeDtypeStruct((count, width), jnp.float32)
        vmem = pl.BlockSpec(memory_space=pltpu.VMEM)
        smem = pl.BlockSpec(memory_space=pltpu.SMEM)
        slots = pltpu.VMEM((devices, count, width), jnp.float32)
        return pl.pallas_call(
            functools.partial(kernel_body, rows, cols),
            out_shape=(block, block),
            in_specs=[vmem, vmem, smem, smem, vmem, vmem],
            out_specs=(vmem, vmem),
            scratch_shapes=[
                pltpu.VMEM((devices, dims, width), jnp.float32),
                slots,
                slots,
                slots,
                pltpu.VMEM((devices * width, width), jnp.bfloat16),
                pltpu.VMEM((devices * width, width), jnp.bfloat16),
                pltpu.VMEM((chips + 2, 1, 128), jnp.float32),
                pltpu.SemaphoreType.DMA((4, chips)),
                pltpu.SemaphoreType.DMA((4, chips)),
                pltpu.SemaphoreType.DMA((4, chips)),
                pltpu.SemaphoreType.DMA((4, chips)),
                pltpu.SemaphoreType.DMA((chips,)),
                pltpu.SemaphoreType.DMA((chips,)),
            ],
            compiler_params=pltpu.CompilerParams(
                collective_id=0, has_side_effects=True, vmem_limit_bytes=60 * 1024 * 1024
            ),
        )(points, lengthscale[None, :], signal, noise, targets[None, :], probe_bits)

    split_points = P(None, ("row", "col"))
    return jax.shard_map(
        body,
        mesh=mesh,
        in_specs=(split_points, P(), P(), P(), P(("row", "col")), split_points),
        out_specs=(split_points, split_points),
        check_vma=False,
    )
```

time: 83.8 us -> 68 us (0.81)
  Pallas kernels: 79.6 us -> 63.8 us
    pallas_call x1, Pallas kernels: 79.6 us -> 63.8 us  [body(): pl.pallas_call(functools.partial(kernel_body, rows, cols), out_shape=(blo...]
where the time goes in v2:
time: 68 us; the launch traced here: 67.7 us
  Pallas kernels  63.8 us (94%)
  local copies, waits for them, and re-layouts  2 us (3%)
  between operations  1.94 us (3%)
    pallas_call x1, Pallas kernels, body(): pl.pallas_call(functools.partial(kernel_body, rows, cols), out_shape=(blo...  63.8 us
    unnamed x4, local copies, waits for them, and re-layouts  2 us

profile of v2, /device:TPU:0, one launch (start us, length us, event | category | flops | bytes accessed | tf_op | source)
XLA Modules:
  0.0 67.7 jit_solution(13552800297596878212)
XLA Ops:
  1.9 63.8 %shard_map.77 = (f32[32,256]{1,0:T(8,128)}, f32[32,256]{1,0:T(8,128)}) custom-call(f32[16,256]{1,0:T(8,128)} %points_ref.1, f32[1,16]{1,0:T(1,128)} %bitcast.3, f32[1]{0:T(128)S(6)} %copy.10.signal_ref, f32[1]{0:T(128)S(6)} %copy.11.noise_ref, f32[1,256]{1,0:T(1,128)} %bitcast.2, s32[31,256]{1,0:T(8,128)} %bits_ref.1), custom_call_target="tpu_custom_call" | custom-call | tf_op jit(solution)/shard_map/pallas_call | solution.py:345
  65.7 0.0 copy-start
  65.7 1.4 %copy.12 = f32[32,256]{1,0:T(8,128)} copy(f32[32,256]{1,0:T(8,128)} %get-tuple-element.4) | data formatting | bytes 65536
  67.1 0.0 copy-done
  67.1 0.6 copy.13
Async XLA Ops:
  65.7 1.4 %copy-start = (f32[32,256]{1,0:T(8,128)S(1)}, f32[32,256]{1,0:T(8,128)}, u32[]{:S(2)}) copy-start(f32[32,256]{1,0:T(8,128)} %get-tuple-element.5) | copy-start | bytes 98308

commit v3 on v2

--- a/solution.py
+++ b/solution.py
@@ -180,18 +180,20 @@
 
     def kernel_tiles(start):
         def run(j, carry):
-            kernel_tile(start + j)
+            kernel_tile(start + 2 * j)
+            kernel_tile(start + 2 * j + 1)
             return carry
 
-        lax.fori_loop(0, chunk, run, 0)
-
-    for c in range(first):
-        forward(POINTS, c)
+        lax.fori_loop(0, chunk // 2, run, 0)
+        if chunk % 2:
+            kernel_tile(start + chunk - 1)
+
+    forward(POINTS, 0)
     for c in range(chunks):
         kernel_tiles(c * chunk)
+        if c + 1 < chunks:
+            forward(POINTS, c + 1)
         forward(RIGHT, c)
-        if first + c < chunks:
-            forward(POINTS, first + c)
     for c in range(chunks):
         arrive_sibling(POINTS, c)
         kernel_tiles(chips + c * chunk)
@@ -240,8 +242,6 @@
     norm_now = total(norm)
     of_residual = summed + noise * vec[0]
     of_direction = of_residual
-    sent_all(POINTS)
-    sent_all(RIGHT)
 
     solved = zero
     residuals = vec
@@ -250,6 +250,9 @@
         images = buffers[phase]
         images[0] = of_direction
         pass_on(phase, 0)
+        if step == 0:
+            sent_all(POINTS)
+            sent_all(RIGHT)
         curved = zero
         product = noise * of_direction
 
@@ -267,9 +270,9 @@
                 curved, product = consume(chips + (c - 1) * chunk, curved, product)
             if first + c < chunks:
                 forward(phase, first + c)
+        sent_all(phase)
         arrive_sibling(phase, chunks - 1)
         curved, product = consume(chips + (chunks - 1) * chunk, curved, product)
-        sent_all(phase)
         alpha = norm_now / total(curved)
         solved = solved + alpha * vec[0]
 

time: 68 us -> 65.1 us (0.957)
  Pallas kernels: 63.8 us -> 60.9 us
    pallas_call x1, Pallas kernels: 63.8 us -> 60.9 us  [body(): pl.pallas_call(functools.partial(kernel_body, rows, cols), out_shape=(blo...]
where the time goes in v3:
time: 65.1 us; the launch traced here: 64.9 us
  Pallas kernels  60.9 us (94%)
  local copies, waits for them, and re-layouts  2 us (3%)
  between operations  1.94 us (3%)
    pallas_call x1, Pallas kernels, body(): pl.pallas_call(functools.partial(kernel_body, rows, cols), out_shape=(blo...  60.9 us
    unnamed x4, local copies, waits for them, and re-layouts  2 us

profile of v3, /device:TPU:0, one launch (start us, length us, event | category | flops | bytes accessed | tf_op | source)
XLA Modules:
  0.0 64.9 jit_solution(9192650342955974791)
XLA Ops:
  1.9 60.9 %shard_map.77 = (f32[32,256]{1,0:T(8,128)}, f32[32,256]{1,0:T(8,128)}) custom-call(f32[16,256]{1,0:T(8,128)} %points_ref.1, f32[1,16]{1,0:T(1,128)} %bitcast.3, f32[1]{0:T(128)S(6)} %copy.10.signal_ref, f32[1]{0:T(128)S(6)} %copy.11.noise_ref, f32[1,256]{1,0:T(1,128)} %bitcast.2, s32[31,256]{1,0:T(8,128)} %bits_ref.1), custom_call_target="tpu_custom_call" | custom-call | tf_op jit(solution)/shard_map/pallas_call | solution.py:348
  62.9 0.0 copy-start
  62.9 1.4 %copy.12 = f32[32,256]{1,0:T(8,128)} copy(f32[32,256]{1,0:T(8,128)} %get-tuple-element.4) | data formatting | bytes 65536
  64.2 0.0 copy-done
  64.2 0.6 copy.13
Async XLA Ops:
  62.9 1.4 %copy-start = (f32[32,256]{1,0:T(8,128)S(1)}, f32[32,256]{1,0:T(8,128)}, u32[]{:S(2)}) copy-start(f32[32,256]{1,0:T(8,128)} %get-tuple-element.5) | copy-start | bytes 98308

commit v4 on v3

--- a/solution.py
+++ b/solution.py
@@ -161,10 +161,6 @@
     c2 = signal * (1.0 / (3.0 * LOG2E * LOG2E))
     across = right_stack(mine)
 
-    pl.semaphore_wait(barrier, chips)
-    pass_on(POINTS, 0)
-    pass_on(RIGHT, 0)
-
     def kernel_tile(slot):
         down = left_stack(pts[slot])
         square = lax.dot_general(
@@ -188,9 +184,18 @@
         if chunk % 2:
             kernel_tile(start + chunk - 1)
 
+    kernel_tile(0)
+    pl.semaphore_wait(barrier, chips)
+    pass_on(POINTS, 0)
+    pass_on(RIGHT, 0)
+
     forward(POINTS, 0)
     for c in range(chunks):
-        kernel_tiles(c * chunk)
+        if c == 0:
+            for k in range(1, chunk):
+                kernel_tile(k)
+        else:
+            kernel_tiles(c * chunk)
         if c + 1 < chunks:
             forward(POINTS, c + 1)
         forward(RIGHT, c)

time: 65.1 us -> 65.3 us (level)
  no operation moved by 1% of the time
where the time goes in v4:
time: 65.3 us; the launch traced here: 65 us
  Pallas kernels  61.1 us (94%)
  local copies, waits for them, and re-layouts  2 us (3%)
  between operations  1.94 us (3%)
    pallas_call x1, Pallas kernels, body(): pl.pallas_call(functools.partial(kernel_body, rows, cols), out_shape=(blo...  61.1 us
    unnamed x4, local copies, waits for them, and re-layouts  2 us

profile of v4, /device:TPU:0, one launch (start us, length us, event | category | flops | bytes accessed | tf_op | source)
XLA Modules:
  0.0 65.0 jit_solution(2725438798110046022)
XLA Ops:
  1.9 61.1 %shard_map.77 = (f32[32,256]{1,0:T(8,128)}, f32[32,256]{1,0:T(8,128)}) custom-call(f32[16,256]{1,0:T(8,128)} %points_ref.1, f32[1,16]{1,0:T(1,128)} %bitcast.3, f32[1]{0:T(128)S(6)} %copy.10.signal_ref, f32[1]{0:T(128)S(6)} %copy.11.noise_ref, f32[1,256]{1,0:T(1,128)} %bitcast.2, s32[31,256]{1,0:T(8,128)} %bits_ref.1), custom_call_target="tpu_custom_call" | custom-call | tf_op jit(solution)/shard_map/pallas_call | solution.py:353
  63.0 0.0 copy-start
  63.0 1.4 %copy.12 = f32[32,256]{1,0:T(8,128)} copy(f32[32,256]{1,0:T(8,128)} %get-tuple-element.4) | data formatting | bytes 65536
  64.4 0.0 copy-done
  64.4 0.6 copy.13
Async XLA Ops:
  63.0 1.4 %copy-start = (f32[32,256]{1,0:T(8,128)S(1)}, f32[32,256]{1,0:T(8,128)}, u32[]{:S(2)}) copy-start(f32[32,256]{1,0:T(8,128)} %get-tuple-element.5) | copy-start | bytes 98308
